TPU v7x, 32 devices: a whole 2x2x4 slice. The times are simulated.
32 devices in a mesh: pts: 32 (over z, y, x, core).
Axes of the slice: x: 2, y: 2, z: 4, core: 2. Of those that a mesh axis runs over, the one named last changes fastest.
Arguments:
- points: bfloat16 [16384, 64], P('pts'), may hold values from -10 to 10, as said below
- targets: float32 [16384], P('pts'), may hold values from -6 to 6
- ridge_weight: float32 [], replicated, may hold values from 0.5 to 4
Outputs:
- coefficients: float32 [16384], P('pts')
- residual: float32 [16384], P('pts')
Inputs may be any that keep to these rules, and one draw needn't show every extreme that they name: `points`: each point lies near one of 341 cluster centres; every coordinate is within -10 and 10.
All inputs are finite; a program needn't handle non-finite values.
Results may differ from a plain program's by a relative error of at most 0.005.
Values may be sent and summed in bfloat16 or wider, within the bound.
A program may use at most 192 MiB of HBM per device.

v0:
```python
import jax
import jax.numpy as jnp
from jax import lax
from jax.sharding import PartitionSpec as P

ITERS = 2


def over_all(shard, axis, dim, absorb, state):
    everything = jax.tree.map(lambda a: lax.all_gather(a, axis, axis=dim, tiled=True), shard)
    return absorb(state, everything, jnp.int32(0))


def kernel_times(own_points, own_norms, shard_rows, coef_part, inverse_width):
    widened = shard_rows.astype(jnp.float32)
    shard_norms = jnp.sum(widened * widened, axis=1)
    cross_term = jnp.dot(own_points, shard_rows.T, preferred_element_type=jnp.float32)
    distance = own_norms[:, None] + shard_norms[None, :] - 2.0 * cross_term
    kernel = jnp.exp(-inverse_width * distance).astype(jnp.bfloat16)
    return jnp.dot(kernel, coef_part, preferred_element_type=jnp.float32)


def apply_operator(direction, points, own_norms, ridge_weight, inverse_width):
    coef_whole = lax.all_gather(direction, "pts", axis=0, tiled=True).astype(jnp.bfloat16)
    local_rows = points.shape[0]
    empty = jnp.zeros((local_rows,), jnp.float32)

    def accumulate(running, shard_rows, first_row):
        coef_part = lax.dynamic_slice_in_dim(coef_whole, first_row, shard_rows.shape[0], 0)
        return running + kernel_times(points, own_norms, shard_rows, coef_part, inverse_width)

    summed = over_all(points, "pts", 0, accumulate, empty)
    return summed + ridge_weight * direction


def body(points, targets, ridge_weight):
    inverse_width = 1.0 / points.shape[1]
    widened = points.astype(jnp.float32)
    own_norms = jnp.sum(widened * widened, axis=1)
    coefficients = jnp.zeros_like(targets)
    residual = targets
    direction = targets
    norm_now = lax.psum(jnp.sum(residual * residual), "pts")
    for iteration in range(ITERS):
        applied = apply_operator(direction, points, own_norms, ridge_weight, inverse_width)
        curvature = lax.psum(jnp.sum(direction * applied), "pts")
        step_size = norm_now / curvature
        coefficients = coefficients + step_size * direction
        residual = residual - step_size * applied
        if iteration + 1 < ITERS:
            norm_next = lax.psum(jnp.sum(residual * residual), "pts")
            direction = residual + norm_next / norm_now * direction
            norm_now = norm_next
    return (coefficients, residual)


def solution(mesh):
    in_specs = (P("pts", None), P("pts"), P())
    out_specs = (P("pts"), P("pts"))
    return jax.shard_map(body, mesh=mesh, in_specs=in_specs, out_specs=out_specs, check_vma=False)
```

profile of v0, /device:TPU:0, one launch (start us, length us, event | category | flops | bytes accessed | tf_op | source)
XLA Modules:
  0.0 273.2 jit_solution(17720178560578662142)
XLA Ops:
  7.2 0.0 all-gather.4.cloned.1.call-start
  7.2 0.7 all-gather.4.cloned.1.call-update
  7.9 0.7 convert
  9.2 43.5 %all-gather = bf16[32,1,512]{2,1,0:T(2,128)(2,1)S(1)} all-gather(bf16[1,1,512]{2,1,0:T(2,128)(2,1)S(1)} %convert), channel_id=1, replica_groups=mesh['pts'=32] {'pts'}, dimensions={0}, use_global_device_ids=true | all-gather | bytes 33792 | tf_op jit(solution)/shard_map/all_gather | solution.py:24
  52.7 0.9 multiply_reduce_fusion.1
  53.6 14.5 %all-gather.4.cloned.1.call-done = bf16[16384,64]{0,1:T(8,128)(2,1)} async-done(((bf16[512,64]{0,1:T(8,128)(2,1)}), bf16[16384,64]{0,1:T(8,128)(2,1)}) %all-gather.4.cloned.1.call-update) | async-done | bytes 2097168 | tf_op jit(solution)/shard_map/all_gather | solution.py:10
  68.1 2.1 multiply_reduce_fusion
  70.2 10.7 %exponential_convert_fusion = bf16[512,16384]{1,0:T(8,128)(2,1)S(1)} fusion(bf16[512,64]{0,1:T(8,128)(2,1)} %param.3, bf16[16384,64]{0,1:T(8,128)(2,1)} %all-gather.4.cloned.1.call-done, f32[16384]{0:T(1024)S(1)} %multiply_reduce_fusion, f32[512]{0:T(512)S(1)} %multiply_reduce_fusion.1), kind=kOutput, calls=%fused_computation | convolution fusion | flops 1115684864 | bytes 19007488 | tf_op jit(solution)/shard_map/dot_general | solution.py:17
  80.9 0.0 copy-start
  80.9 0.0 copy-start.1
  80.9 5.7 %copy-done = bf16[512,16384]{1,0:T(8,128)(2,1)} copy-done((bf16[512,16384]{1,0:T(8,128)(2,1)}, bf16[512,16384]{1,0:T(8,128)(2,1)S(1)}, u32[]{:S(2)}) %copy-start) | copy-done | bytes 16777240
  86.6 4.4 %fusion = f32[1,512]{1,0:T(1,128)S(1)} fusion(bf16[512,16384]{1,0:T(8,128)(2,1)S(1)} %exponential_convert_fusion, bf16[16384,1]{0,1:T(2,128)(2,1)S(1)} %bitcast.12), kind=kOutput, calls=%fused_computation.13 | convolution fusion | flops 16777216 | bytes 16812032 | tf_op jit(solution)/shard_map/dot_general | solution.py:20
  91.0 0.0 copy-done.1
  91.0 0.6 multiply_reduce_fusion.4
  91.7 40.0 %all-reduce = (f32[]{:T(128)}, f32[]{:T(128)}) all-reduce(f32[]{:T(128)} %get-tuple-element.3, f32[]{:T(128)} %get-tuple-element.2), channel_id=1, replica_groups=mesh['pts'=32] {'pts'}, use_global_device_ids=true, to_apply=%region_1.0 | all-reduce | flops 2 | bytes 16 | tf_op jit(solution)/shard_map/psum | solution.py:43
  133.0 0.6 multiply_reduce_fusion.3
  133.6 40.0 %psum.30 = f32[]{:T(128)} all-reduce(f32[]{:T(128)} %multiply_reduce_fusion.3), channel_id=1, replica_groups=mesh['pts'=32] {'pts'}, use_global_device_ids=true, to_apply=%region_7.0 | all-reduce | flops 1 | bytes 8 | tf_op jit(solution)/shard_map/psum | solution.py:51
  175.0 41.6 %all-gather.1 = bf16[32,1,512]{2,1,0:T(2,128)(2,1)S(1)} all-gather(bf16[1,1,512]{2,1,0:T(2,128)(2,1)S(1)} %convert.1), channel_id=1, replica_groups=mesh['pts'=32] {'pts'}, dimensions={0}, use_global_device_ids=true | all-gather | bytes 33792 | tf_op jit(solution)/shard_map/all_gather | solution.py:24
  216.6 10.2 %fusion.1 = f32[1,512]{1,0:T(1,128)S(1)} fusion(bf16[512,16384]{1,0:T(8,128)(2,1)} %copy-done, bf16[16384,1]{0,1:T(2,128)(2,1)S(1)} %bitcast.13), kind=kOutput, calls=%fused_computation.14 | convolution fusion | flops 16777216 | bytes 16812032 | tf_op jit(solution)/shard_map/dot_general | solution.py:20
  226.8 0.6 multiply_reduce_fusion.2
  227.4 37.0 %psum.31 = f32[]{:T(128)} all-reduce(f32[]{:T(128)} %multiply_reduce_fusion.2), channel_id=1, replica_groups=mesh['pts'=32] {'pts'}, use_global_device_ids=true, to_apply=%region_9.0 | all-reduce | flops 1 | bytes 8 | tf_op jit(solution)/shard_map/psum | solution.py:46
  265.8 0.6 multiply_subtract_fusion
  (2 shorter events, 0.0 us)
Async XLA Ops:
  7.2 60.9 %all-gather.4.cloned.1.call-start = ((), (), s32[]{:S(2)}) async-start(), calls=%async_computation | async-start | bytes 2162688 | tf_op jit(solution)/shard_map/all_gather | solution.py:10
  80.9 5.7 %copy-start = (bf16[512,16384]{1,0:T(8,128)(2,1)}, bf16[512,16384]{1,0:T(8,128)(2,1)S(1)}, u32[]{:S(2)}) copy-start(bf16[512,16384]{1,0:T(8,128)(2,1)S(1)} %exponential_convert_fusion) | copy-start | bytes 50331652
  80.9 10.1 %copy-start.1 = (f32[512]{0:T(512)S(1)}, f32[512]{0:T(512)}, u32[]{:S(2)}) copy-start(f32[512]{0:T(512)} %param.4) | copy-start | bytes 6148
Sparse Core Ops, SparseCore 0:
  10.9 57.1 all-gather.3
where the time goes:
time: 275 us; the launch traced here: 273 us
  blocking collectives  202 us (73%)
  matrix products  25.3 us (9%)
  between operations  18.7 us (7%)
  waiting for transfers between devices  15.2 us (6%)
  other arithmetic  6.12 us (2%)
  local copies, waits for them, and re-layouts  5.7 us (2%)
    all_gather x2, blocking collectives, apply_operator(): lax.all_gather(direction, 'pts', axis=0, tiled=True).astype(jnp.bfloat16)  85 us
    psum x1, blocking collectives, body(): norm_now = lax.psum(jnp.sum(residual * residual), 'pts')  40 us
    psum x1, blocking collectives, body(): norm_next = lax.psum(jnp.sum(residual * residual), 'pts')  40 us
    psum x1, blocking collectives, body(): curvature = lax.psum(jnp.sum(direction * applied), 'pts')  37 us
    dot_general x2, matrix products, kernel_times(): return jnp.dot(kernel, coef_part, preferred_element_type=jnp.float32)  14.6 us
    all_gather x1, waiting for transfers between devices, over_all(): lax.all_gather(a, axis, axis=dim, tiled=True)  14.5 us
    dot_general x1, matrix products, kernel_times(): jnp.dot(own_points, shard_rows.T, preferred_element_type=jnp.float32)  10.7 us
    unnamed x4, local copies, waits for them, and re-layouts  5.7 us
  transfers between devices with their start and end apart: 1, of which 1 were waited for; matrix products, arithmetic and copies ran while one was open for 1% of the time, Pallas kernels for 0%

commit v1 on v0

v1 whole, which is shorter than its diff:
```python
import functools

import jax
import jax.numpy as jnp
from jax import lax
from jax.experimental import pallas as pl
from jax.experimental.pallas import tpu as pltpu
from jax.sharding import PartitionSpec as P

F32 = jnp.float32
BF16 = jnp.bfloat16
KEEP_BYTES = 40 * 1024 * 1024


def kernel(n, dim, keep, pts, tgt, ridge, coef_out, res_out, mine, blocks, t_all, w_all,
           c_all, r_a, r_b, kt, sem_ts, sem_tr, sem_ps, sem_pr, sem_fs, sem_fr, sem_ws,
           sem_wr, sem_cs, sem_cr):
    me = lax.axis_index("pts")
    half_n = n // 2
    core = lax.rem(me, 2)
    partner = me + 1 - 2 * core
    local = tgt.shape[1]
    half = local // 2
    wide = 2 * dim

    def same(k):
        return lax.rem(me + 2 * k, n)

    def other(k):
        d = lax.rem(me + 2 * k, n)
        return d + 1 - 2 * lax.rem(d, 2)

    barrier = pltpu.get_barrier_semaphore()

    @pl.loop(1, n)
    def _(k):
        pl.semaphore_signal(barrier, inc=1, device_id=(lax.rem(me + k, n),),
                            device_id_type=pl.DeviceIdType.MESH)

    own = pts[...].astype(F32)
    packed = jnp.concatenate([own[:half], own[half:]], axis=1).astype(BF16)
    mine[...] = packed
    own_t = own.T
    s_row = jnp.sum(own_t * own_t, axis=0, keepdims=True) * (-1.0 / dim)
    s_hi = s_row.astype(BF16).astype(F32)
    s_mid = (s_row - s_hi).astype(BF16).astype(F32)
    s_lo = s_row - s_hi - s_mid
    rows = lax.broadcasted_iota(jnp.int32, (dim, local), 0)
    pieces = jnp.where(rows == 0, s_hi, jnp.where(rows == 1, s_mid, jnp.where(rows == 2, s_lo, 0.0)))
    pieces = pieces.astype(BF16)
    scaled = (own_t * (2.0 / dim)).astype(BF16)
    minus = jnp.full((dim, local), -1.0 / dim, BF16)
    r_a[0:dim] = scaled
    r_a[dim:2 * dim] = minus
    r_a[2 * dim:3 * dim] = minus
    r_a[3 * dim:4 * dim] = pieces
    r_b[0:dim] = minus
    r_b[dim:2 * dim] = scaled
    r_b[2 * dim:3 * dim] = pieces
    r_b[3 * dim:4 * dim] = minus

    def send(src, dst, ssem, rsem, dev):
        return pltpu.make_async_remote_copy(
            src_ref=src, dst_ref=dst, send_sem=ssem, recv_sem=rsem,
            device_id=(dev,), device_id_type=pl.DeviceIdType.MESH)

    def t_copy(p, k):
        return send(tgt, t_all.at[p, k], sem_ts.at[p, k], sem_tr.at[p, k], other(k) if p else same(k))

    def w_copy(p, k):
        return send(w_all.at[0, 0], w_all.at[p, k], sem_ws.at[p, k], sem_wr.at[p, k], other(k) if p else same(k))

    def c_copy(p, k):
        return send(c_all.at[0, 0], c_all.at[p, k], sem_cs.at[p, k], sem_cr.at[p, k], other(k) if p else same(k))

    def p_copy(k):
        return send(mine, blocks.at[0, k], sem_ps.at[k], sem_pr.at[k], same(k))

    def f_first():
        return send(mine, blocks.at[1, 0], sem_fs.at[0], sem_fr.at[0], partner)

    def f_copy(k):
        return send(blocks.at[0, k], blocks.at[1, k], sem_fs.at[k], sem_fr.at[k], partner)

    def each(fn):
        fn(1, 0)

        @pl.loop(1, half_n)
        def _(k):
            fn(0, k)
            fn(1, k)

    pl.semaphore_wait(barrier, n - 1)
    f_first().start()

    @pl.loop(1, half_n)
    def _(k):
        p_copy(k).start()

    each(lambda p, k: t_copy(p, k).start())
    t_all[0, 0] = tgt[...]

    lanes = lax.broadcasted_iota(jnp.int32, (half, wide), 1)
    first = lanes < dim
    one = jnp.ones((half, wide), BF16)

    def tile(pb):
        f = pb.astype(F32)
        sq = f * f
        hi = sq.astype(BF16)
        lo = (sq - hi.astype(F32)).astype(BF16)
        hi = pltpu.roll(hi.astype(F32), dim, 1).astype(BF16)
        top = jnp.concatenate([jnp.where(first, pb, hi), jnp.where(first, lo, one)], axis=1)
        bot = jnp.concatenate([jnp.where(first, hi, pb), jnp.where(first, one, lo)], axis=1)
        e_top = jnp.dot(top, r_a[...], preferred_element_type=F32)
        k_top = jnp.exp(e_top).astype(BF16)
        e_bot = jnp.dot(bot, r_b[...], preferred_element_type=F32)
        k_bot = jnp.exp(e_bot).astype(BF16)
        return k_top, k_bot

    def absorb(pb, p, k, vec, acc):
        k_top, k_bot = tile(pb)
        if keep:
            kt[p, k, 0:half] = k_top
            kt[p, k, half:local] = k_bot
        v = vec.astype(BF16)
        acc = acc + jnp.dot(v[:, :half], k_top, preferred_element_type=F32)
        return acc + jnp.dot(v[:, half:], k_bot, preferred_element_type=F32)

    acc = jnp.zeros((1, local), F32)
    acc = absorb(mine[...], 0, 0, tgt[...], acc)
    f_first().wait_recv()
    t_copy(1, 0).wait_recv()
    acc = absorb(blocks[1, 0], 1, 0, t_all[1, 0], acc)

    def step(k, acc):
        p_copy(k).wait_recv()
        f_copy(k).start()
        t_copy(0, k).wait_recv()
        acc = absorb(blocks[0, k], 0, k, t_all[0, k], acc)
        f_copy(k).wait_recv()
        t_copy(1, k).wait_recv()
        return absorb(blocks[1, k], 1, k, t_all[1, k], acc)

    acc = lax.fori_loop(1, half_n, step, acc)
    weight = ridge[0, 0]
    w_all[0, 0] = acc + weight * tgt[...]
    t_whole = t_all[...]
    norm0 = jnp.sum(t_whole * t_whole)
    each(lambda p, k: w_copy(p, k).start())

    f_first().wait_send()

    @pl.loop(1, half_n)
    def _(k):
        p_copy(k).wait_send()
        f_copy(k).wait_send()

    each(lambda p, k: t_copy(p, k).wait_send())
    each(lambda p, k: w_copy(p, k).wait_recv())
    each(lambda p, k: w_copy(p, k).wait_send())
    w_whole = w_all[...]
    step0 = norm0 / jnp.sum(t_whole * w_whole)
    r1 = t_whole - step0 * w_whole
    norm1 = jnp.sum(r1 * r1)
    d1 = r1 + (norm1 / norm0) * t_whole
    t_all[...] = d1

    def again(k, acc):
        for p in (0, 1):
            if keep:
                acc = acc + jnp.dot(t_all[p, k].astype(BF16), kt[p, k], preferred_element_type=F32)
            else:
                acc = absorb(blocks[p, k], p, k, t_all[p, k], acc)
        return acc

    if not keep:
        blocks[0, 0] = mine[...]
    acc = lax.fori_loop(0, half_n, again, jnp.zeros((1, local), F32))
    d_own = t_all[0, 0]
    applied = acc + weight * d_own
    part = jnp.sum(d_own * applied)
    c_all[0, 0] = jnp.full((1, 128), part, F32)
    each(lambda p, k: c_copy(p, k).start())
    each(lambda p, k: c_copy(p, k).wait_recv())
    each(lambda p, k: c_copy(p, k).wait_send())
    curvature = jnp.sum(jnp.sum(c_all[...], axis=(0, 1)), axis=0, keepdims=True)[:, 0:1]
    step1 = norm1 / curvature
    coef_out[...] = step0 * tgt[...] + step1 * d_own
    res_out[...] = tgt[...] - step0 * w_all[0, 0] - step1 * applied


def body(n, points, targets, ridge_weight):
    local, dim = points.shape
    half_n = n // 2
    keep = n * local * local * 2 <= KEEP_BYTES
    kt_shape = (2, half_n, local, local) if keep else (1, 1, 16, 128)
    dma = pltpu.SemaphoreType.DMA
    vec = jax.ShapeDtypeStruct((1, local), F32)
    coef, res = pl.pallas_call(
        functools.partial(kernel, n, dim, keep),
        out_shape=(vec, vec),
        in_specs=[
            pl.BlockSpec(memory_space=pltpu.VMEM),
            pl.BlockSpec(memory_space=pltpu.VMEM),
            pl.BlockSpec(memory_space=pltpu.SMEM),
        ],
        out_specs=(pl.BlockSpec(memory_space=pltpu.VMEM), pl.BlockSpec(memory_space=pltpu.VMEM)),
        scratch_shapes=[
            pltpu.VMEM((local // 2, 2 * dim), BF16),
            pltpu.VMEM((2, half_n, local // 2, 2 * dim), BF16),
            pltpu.VMEM((2, half_n, 1, local), F32),
            pltpu.VMEM((2, half_n, 1, local), F32),
            pltpu.VMEM((2, half_n, 1, 128), F32),
            pltpu.VMEM((4 * dim, local), BF16),
            pltpu.VMEM((4 * dim, local), BF16),
            pltpu.VMEM(kt_shape, BF16),
            dma((2, half_n)), dma((2, half_n)),
            dma((half_n,)), dma((half_n,)),
            dma((half_n,)), dma((half_n,)),
            dma((2, half_n)), dma((2, half_n)),
            dma((2, half_n)), dma((2, half_n)),
        ],
        compiler_params=pltpu.CompilerParams(
            collective_id=0, has_side_effects=True, vmem_limit_bytes=60 * 1024 * 1024),
    )(points, targets.reshape(1, local), ridge_weight.reshape(1, 1))
    return coef.reshape(local), res.reshape(local)


def solution(mesh):
    n = mesh.shape["pts"]
    return jax.shard_map(
        functools.partial(body, n), mesh=mesh,
        in_specs=(P("pts", None), P("pts"), P()),
        out_specs=(P("pts"), P("pts")), check_vma=False)
```

time: 275 us -> 75.8 us (0.28)
  blocking collectives: 202 us -> 0 us
  Pallas kernels: 0 us -> 70.8 us
  matrix products: 25.3 us -> 0 us
  between operations: 18.7 us -> 1.29 us
  waiting for transfers between devices: 15.2 us -> 0 us
  other arithmetic: 6.12 us -> 0 us
    psum x3 -> x0, blocking collectives: 117 us -> none  [the longest x1 40 us: body(): norm_now = lax.psum(jnp.sum(residual * residual), 'pts')]
    all_gather x2 -> x0, blocking collectives: 85 us -> none  [apply_operator(): lax.all_gather(direction, 'pts', axis=0, tiled=True).astype(jnp.bfloat16)]
    pallas_call x0 -> x1, Pallas kernels: none -> 70.8 us  [body(): pl.pallas_call(functools.partial(kernel, n, dim, keep), out_shape=(vec, v...]
    dot_general x3 -> x0, matrix products: 25.3 us -> none  [the longest x2 14.6 us: kernel_times(): return jnp.dot(kernel, coef_part, preferred_element_type=jnp.float32)]
    all_gather x1 -> x0, waiting for transfers between devices: 14.5 us -> none  [over_all(): lax.all_gather(a, axis, axis=dim, tiled=True)]
    reduce_sum x5 -> x0, other arithmetic: 4.83 us -> none  [the longest x1 2.11 us: kernel_times(): shard_norms = jnp.sum(widened * widened, axis=1)]
    unnamed x4 -> x7, local copies, waits for them, and re-layouts: 5.7 us -> 3.49 us
  transfers between devices with their start and end apart: 1 -> 0, of which waited for: 1 -> 0; matrix products, arithmetic and copies ran while one was open for 1% -> 0% of each run, Pallas kernels for 0% -> 0%
where the time goes in v1:
time: 75.8 us; the launch traced here: 75.6 us
  Pallas kernels  70.8 us (93%)
  local copies, waits for them, and re-layouts  3.49 us (5%)
  between operations  1.29 us (2%)
    pallas_call x1, Pallas kernels, body(): pl.pallas_call(functools.partial(kernel, n, dim, keep), out_shape=(vec, v...  70.8 us
    unnamed x7, local copies, waits for them, and re-layouts  3.49 us

profile of v1, /device:TPU:0, one launch (start us, length us, event | category | flops | bytes accessed | tf_op | source)
XLA Modules:
  0.0 75.6 jit_solution(6393080686319421576)
XLA Ops:
  1.3 1.6 %copy.5.pts = bf16[512,64]{1,0:T(8,128)(2,1)} copy(bf16[512,64]{0,1:T(8,128)(2,1)} %param.3) | data formatting | bytes 131072 | tf_op args[0]
  2.9 70.8 %shard_map.50 = (f32[1,512]{1,0:T(1,128)}, f32[1,512]{1,0:T(1,128)}) custom-call(bf16[512,64]{1,0:T(8,128)(2,1)} %copy.5.pts, f32[1,512]{1,0:T(1,128)} %bitcast.5, f32[1,1]{1,0:T(1,128)} %bitcast.4.ridge), custom_call_target="tpu_custom_call" | custom-call | tf_op jit(solution)/shard_map/pallas_call | solution.py:200
  73.7 0.0 copy-start.1
  73.7 0.7 copy-done.1
  74.3 0.0 copy-start
  74.3 0.6 copy.9
  74.9 0.1 copy-done
  75.0 0.6 copy.10
Async XLA Ops:
  73.7 0.7 copy-start.1
  74.3 0.7 copy-start

commit v2 on v1

v2 whole, which is shorter than its diff:
```python
import functools

import jax
import jax.numpy as jnp
from jax import lax
from jax.experimental import pallas as pl
from jax.experimental.pallas import tpu as pltpu
from jax.sharding import PartitionSpec as P

F32 = jnp.float32
BF16 = jnp.bfloat16
KEEP_BYTES = 40 * 1024 * 1024


def kernel(n, dim, keep, pts_hbm, tgt, ridge, coef_out, res_out, pts, blocks, t_all, w_all,
           c_all, r_a, r_b, kt, sem_in, sem_ps, sem_pr, sem_fs, sem_fr, sem_ws,
           sem_wr, sem_gs, sem_gr, sem_cs, sem_cr):
    me = lax.axis_index("pts")
    half_n = n // 2
    stages = half_n.bit_length() - 1
    local = tgt.shape[1]
    half = local // 2
    wide = 2 * dim
    t_rows = local // wide

    def device(p, q):
        d = lax.rem(me + p, 2)
        for s in range(stages):
            bit = half_n >> s
            d = d + lax.rem(me // bit + q // (1 << s), 2) * bit
        return d

    partner = device(1, 0)
    load = pltpu.make_async_copy(pts_hbm, pts, sem_in)
    load.start()
    barrier = pltpu.get_barrier_semaphore()
    for dev in [partner] + [device(0, 1 << s) for s in range(stages)]:
        pl.semaphore_signal(barrier, inc=1, device_id=(dev,), device_id_type=pl.DeviceIdType.MESH)

    target = tgt[...]
    t_hi = target.astype(BF16)
    t_rest = target - t_hi.astype(F32)
    t_mid = t_rest.astype(BF16)
    t_lo = (t_rest - t_mid.astype(F32)).astype(BF16)
    cut = [part.astype(F32)[:, i * wide:(i + 1) * wide] for part in (t_hi, t_mid, t_lo) for i in range(t_rows)]
    pad = -len(cut) % 16
    t_tile = jnp.concatenate(cut + [jnp.zeros((pad, wide), F32)], axis=0).astype(BF16)
    load.wait()
    own = pts[...].astype(F32)
    blocks[0, 0, 0:half] = jnp.concatenate([own[:half], own[half:]], axis=1).astype(BF16)
    blocks[0, 0, half:] = t_tile
    t_all[0, 0] = target
    own_t = own.T
    s_row = jnp.sum(own_t * own_t, axis=0, keepdims=True) * (-1.0 / dim)
    s_hi = s_row.astype(BF16).astype(F32)
    s_mid = (s_row - s_hi).astype(BF16).astype(F32)
    s_lo = s_row - s_hi - s_mid
    rows = lax.broadcasted_iota(jnp.int32, (dim, local), 0)
    pieces = jnp.where(rows == 0, s_hi, jnp.where(rows == 1, s_mid, jnp.where(rows == 2, s_lo, 0.0)))
    pieces = pieces.astype(BF16)
    scaled = (own_t * (2.0 / dim)).astype(BF16)
    minus = jnp.full((dim, local), -1.0 / dim, BF16)
    r_a[0:dim] = scaled
    r_a[dim:2 * dim] = minus
    r_a[2 * dim:3 * dim] = minus
    r_a[3 * dim:4 * dim] = pieces
    r_b[0:dim] = minus
    r_b[dim:2 * dim] = scaled
    r_b[2 * dim:3 * dim] = pieces
    r_b[3 * dim:4 * dim] = minus

    def send(src, dst, ssem, rsem, dev):
        return pltpu.make_async_remote_copy(
            src_ref=src, dst_ref=dst, send_sem=ssem, recv_sem=rsem,
            device_id=(dev,), device_id_type=pl.DeviceIdType.MESH)

    def w_copy(q):
        return send(w_all.at[0, 0], w_all.at[0, q], sem_ws.at[q], sem_wr.at[q], device(0, q))

    def g_copy(q):
        return send(w_all.at[0, q], w_all.at[1, q], sem_gs.at[q], sem_gr.at[q], partner)

    def c_copy(p, q):
        return send(c_all.at[0, 0], c_all.at[p, q], sem_cs.at[p, q], sem_cr.at[p, q], device(p, q))

    def p_copy(q, s):
        to = q + (1 << s)
        return send(blocks.at[0, q], blocks.at[0, to], sem_ps.at[to], sem_pr.at[to], device(0, 1 << s))

    def p_from(q):
        return send(blocks.at[0, 0], blocks.at[0, q], sem_ps.at[q], sem_pr.at[q], partner)

    def f_copy(q):
        return send(blocks.at[0, q], blocks.at[1, q], sem_fs.at[q], sem_fr.at[q], partner)

    def each(fn):
        fn(1, 0)

        @pl.loop(1, half_n)
        def _(q):
            fn(0, q)
            fn(1, q)

    pl.semaphore_wait(barrier, stages + 1)
    for s in reversed(range(stages)):
        p_copy(0, s).start()
    f_copy(0).start()

    lanes = lax.broadcasted_iota(jnp.int32, (half, wide), 1)
    first = lanes < dim
    one = jnp.ones((half, wide), BF16)

    def tile(pb):
        f = pb.astype(F32)
        sq = f * f
        hi = sq.astype(BF16)
        lo = (sq - hi.astype(F32)).astype(BF16)
        hi = pltpu.roll(hi.astype(F32), dim, 1).astype(BF16)
        top = jnp.concatenate([jnp.where(first, pb, hi), jnp.where(first, lo, one)], axis=1)
        bot = jnp.concatenate([jnp.where(first, hi, pb), jnp.where(first, one, lo)], axis=1)
        e_top = jnp.dot(top, r_a[...], preferred_element_type=F32)
        k_top = jnp.exp(e_top).astype(BF16)
        e_bot = jnp.dot(bot, r_b[...], preferred_element_type=F32)
        k_bot = jnp.exp(e_bot).astype(BF16)
        return k_top, k_bot

    def absorb(p, q, vec, acc):
        k_top, k_bot = tile(blocks[p, q, 0:half])
        if keep:
            kt[p, q, 0:half] = k_top
            kt[p, q, half:local] = k_bot
        v = vec.astype(BF16)
        acc = acc + jnp.dot(v[:, :half], k_top, preferred_element_type=F32)
        return acc + jnp.dot(v[:, half:], k_bot, preferred_element_type=F32)

    def unpack(p, q):
        part = blocks[p, q, half:].astype(F32)
        hi, mid, lo = (
            jnp.concatenate([part[i * t_rows + j:i * t_rows + j + 1] for j in range(t_rows)], axis=1)
            for i in range(3))
        vec = hi + mid + lo
        t_all[p, q] = vec
        return vec

    acc = jnp.zeros((1, local), F32)
    acc = absorb(0, 0, target, acc)
    f_copy(0).wait_recv()
    acc = absorb(1, 0, unpack(1, 0), acc)

    def step(q, acc):
        p_from(q).wait_recv()
        for s in reversed(range(stages)):
            @pl.when(q < (1 << s))
            def _():
                p_copy(q, s).start()
        f_copy(q).start()
        acc = absorb(0, q, unpack(0, q), acc)
        f_copy(q).wait_recv()
        return absorb(1, q, unpack(1, q), acc)

    acc = lax.fori_loop(1, half_n, step, acc)
    weight = ridge[0, 0]
    w_all[0, 0] = acc + weight * target
    t_whole = t_all[...]
    norm0 = jnp.sum(t_whole * t_whole)
    g_copy(0).start()

    @pl.loop(1, half_n)
    def _(q):
        w_copy(q).start()

    f_copy(0).wait_send()

    @pl.loop(1, half_n)
    def _(q):
        p_from(q).wait_send()
        f_copy(q).wait_send()

    @pl.loop(1, half_n)
    def _(q):
        w_copy(q).wait_recv()
        g_copy(q).start()

    @pl.loop(1, half_n)
    def _(q):
        w_copy(q).wait_send()

    @pl.loop(0, half_n)
    def _(q):
        g_copy(q).wait()

    w_whole = w_all[...]
    step0 = norm0 / jnp.sum(t_whole * w_whole)
    r1 = t_whole - step0 * w_whole
    norm1 = jnp.sum(r1 * r1)
    d1 = r1 + (norm1 / norm0) * t_whole
    t_all[...] = d1

    def again(q, acc):
        for p in (0, 1):
            if keep:
                acc = acc + jnp.dot(t_all[p, q].astype(BF16), kt[p, q], preferred_element_type=F32)
            else:
                acc = absorb(p, q, t_all[p, q], acc)
        return acc

    acc = lax.fori_loop(0, half_n, again, jnp.zeros((1, local), F32))
    d_own = t_all[0, 0]
    applied = acc + weight * d_own
    part = jnp.sum(d_own * applied)
    c_all[0, 0] = jnp.full((1, 128), part, F32)
    each(lambda p, q: c_copy(p, q).start())
    each(lambda p, q: c_copy(p, q).wait_recv())
    each(lambda p, q: c_copy(p, q).wait_send())
    curvature = jnp.sum(jnp.sum(c_all[...], axis=(0, 1)), axis=0, keepdims=True)[:, 0:1]
    step1 = norm1 / curvature
    coef_out[...] = step0 * target + step1 * d_own
    res_out[...] = target - step0 * w_all[0, 0] - step1 * applied


def body(n, points, targets, ridge_weight):
    local, dim = points.shape
    half_n = n // 2
    keep = n * local * local * 2 <= KEEP_BYTES
    kt_shape = (2, half_n, local, local) if keep else (1, 1, 16, 128)
    t_tile = -(-3 * local // (32 * dim)) * 16
    dma = pltpu.SemaphoreType.DMA
    vec = jax.ShapeDtypeStruct((1, local), F32)
    coef, res = pl.pallas_call(
        functools.partial(kernel, n, dim, keep),
        out_shape=(vec, vec),
        in_specs=[
            pl.BlockSpec(memory_space=pl.ANY),
            pl.BlockSpec(memory_space=pltpu.VMEM),
            pl.BlockSpec(memory_space=pltpu.SMEM),
        ],
        out_specs=(pl.BlockSpec(memory_space=pltpu.VMEM), pl.BlockSpec(memory_space=pltpu.VMEM)),
        scratch_shapes=[
            pltpu.VMEM((local, dim), BF16),
            pltpu.VMEM((2, half_n, local // 2 + t_tile, 2 * dim), BF16),
            pltpu.VMEM((2, half_n, 1, local), F32),
            pltpu.VMEM((2, half_n, 1, local), F32),
            pltpu.VMEM((2, half_n, 1, 128), F32),
            pltpu.VMEM((4 * dim, local), BF16),
            pltpu.VMEM((4 * dim, local), BF16),
            pltpu.VMEM(kt_shape, BF16),
            dma,
            dma((half_n,)), dma((half_n,)),
            dma((half_n,)), dma((half_n,)),
            dma((half_n,)), dma((half_n,)),
            dma((half_n,)), dma((half_n,)),
            dma((2, half_n)), dma((2, half_n)),
        ],
        compiler_params=pltpu.CompilerParams(
            collective_id=0, has_side_effects=True, vmem_limit_bytes=60 * 1024 * 1024),
    )(points, targets.reshape(1, local), ridge_weight.reshape(1, 1))
    return coef.reshape(local), res.reshape(local)


def solution(mesh):
    n = mesh.shape["pts"]
    return jax.shard_map(
        functools.partial(body, n), mesh=mesh,
        in_specs=(P("pts", None), P("pts"), P()),
        out_specs=(P("pts"), P("pts")), check_vma=False)
```

time: 75.8 us -> 55.3 us (0.73)
  Pallas kernels: 70.8 us -> 50.2 us
    pallas_call x1, Pallas kernels: 70.8 us -> 50.2 us  [body(): pl.pallas_call(functools.partial(kernel, n, dim, keep), out_shape=(vec, v...]
where the time goes in v2:
time: 55.3 us; the launch traced here: 55 us
  Pallas kernels  50.2 us (91%)
  local copies, waits for them, and re-layouts  3.49 us (6%)
  between operations  1.29 us (2%)
    pallas_call x1, Pallas kernels, body(): pl.pallas_call(functools.partial(kernel, n, dim, keep), out_shape=(vec, v...  50.2 us
    unnamed x7, local copies, waits for them, and re-layouts  3.49 us

profile of v2, /device:TPU:0, one launch (start us, length us, event | category | flops | bytes accessed | tf_op | source)
XLA Modules:
  0.0 55.0 jit_solution(13258168724574975729)
XLA Ops:
  1.3 1.6 %copy.5.pts_hbm = bf16[512,64]{1,0:T(8,128)(2,1)} copy(bf16[512,64]{0,1:T(8,128)(2,1)} %param.3) | data formatting | bytes 131072 | tf_op args[0]
  2.9 50.2 %shard_map.50 = (f32[1,512]{1,0:T(1,128)}, f32[1,512]{1,0:T(1,128)}) custom-call(bf16[512,64]{1,0:T(8,128)(2,1)} %copy.5.pts_hbm, f32[1,512]{1,0:T(1,128)} %bitcast.5, f32[1,1]{1,0:T(1,128)} %bitcast.4.ridge), custom_call_target="tpu_custom_call" | custom-call | tf_op jit(solution)/shard_map/pallas_call | solution.py:229
  53.1 0.0 copy-start.1
  53.1 0.7 %copy-done.1 = f32[1,512]{1,0:T(1,128)S(1)} copy-done((f32[1,512]{1,0:T(1,128)S(1)}, f32[1,512]{1,0:T(1,128)}, u32[]{:S(2)}) %copy-start.1) | copy-done | bytes 2072
  53.8 0.0 copy-start
  53.8 0.6 %copy.9 = f32[512]{0:T(512)} copy(f32[512]{0:T(512)S(1)} %bitcast.7) | data formatting | bytes 4096
  54.3 0.1 copy-done
  54.4 0.6 %copy.10 = f32[512]{0:T(512)} copy(f32[512]{0:T(512)S(1)} %bitcast.6) | data formatting | bytes 4096
Async XLA Ops:
  53.1 0.7 %copy-start.1 = (f32[1,512]{1,0:T(1,128)S(1)}, f32[1,512]{1,0:T(1,128)}, u32[]{:S(2)}) copy-start(f32[1,512]{1,0:T(1,128)} %get-tuple-element.4) | copy-start | bytes 6148
  53.8 0.7 %copy-start = (f32[1,512]{1,0:T(1,128)S(1)}, f32[1,512]{1,0:T(1,128)}, u32[]{:S(2)}) copy-start(f32[1,512]{1,0:T(1,128)} %get-tuple-element.5) | copy-start | bytes 6148

commit v3 on v2

--- a/solution.py
+++ b/solution.py
@@ -20,8 +20,10 @@
     stages = half_n.bit_length() - 1
     local = tgt.shape[1]
     half = local // 2
+    quarter = local // 4
     wide = 2 * dim
-    t_rows = local // wide
+    t_rows = quarter // wide
+    low = half_n // 4
 
     def device(p, q):
         d = lax.rem(me + p, 2)
@@ -30,6 +32,14 @@
             d = d + lax.rem(me // bit + q // (1 << s), 2) * bit
         return d
 
+    def stage_bit(z, s):
+        if z and s >= stages - 2:
+            s = 2 * stages - 3 - s
+        return 1 << s
+
+    def swapped(q):
+        return q - low * (lax.rem(q // (2 * low), 2) - lax.rem(q // low, 2))
+
     partner = device(1, 0)
     load = pltpu.make_async_copy(pts_hbm, pts, sem_in)
     load.start()
@@ -42,14 +52,20 @@
     t_rest = target - t_hi.astype(F32)
     t_mid = t_rest.astype(BF16)
     t_lo = (t_rest - t_mid.astype(F32)).astype(BF16)
-    cut = [part.astype(F32)[:, i * wide:(i + 1) * wide] for part in (t_hi, t_mid, t_lo) for i in range(t_rows)]
-    pad = -len(cut) % 16
-    t_tile = jnp.concatenate(cut + [jnp.zeros((pad, wide), F32)], axis=0).astype(BF16)
+    parts = [part.astype(F32) for part in (t_hi, t_mid, t_lo)]
+
+    def t_tile(z):
+        cut = [part[:, i:i + wide] for part in parts for h in (0, half)
+               for i in range(h + z * quarter, h + (z + 1) * quarter, wide)]
+        pad = -len(cut) % 16
+        return jnp.concatenate(cut + [jnp.zeros((pad, wide), F32)], axis=0).astype(BF16)
+
     load.wait()
     own = pts[...].astype(F32)
-    blocks[0, 0, 0:half] = jnp.concatenate([own[:half], own[half:]], axis=1).astype(BF16)
-    blocks[0, 0, half:] = t_tile
-    t_all[0, 0] = target
+    packed = jnp.concatenate([own[:half], own[half:]], axis=1).astype(BF16)
+    for z in (0, 1):
+        blocks[0, 0, z, 0:quarter] = packed[z * quarter:(z + 1) * quarter]
+        blocks[0, 0, z, quarter:] = t_tile(z)
     own_t = own.T
     s_row = jnp.sum(own_t * own_t, axis=0, keepdims=True) * (-1.0 / dim)
     s_hi = s_row.astype(BF16).astype(F32)
@@ -83,15 +99,16 @@
     def c_copy(p, q):
         return send(c_all.at[0, 0], c_all.at[p, q], sem_cs.at[p, q], sem_cr.at[p, q], device(p, q))
 
-    def p_copy(q, s):
+    def p_copy(z, q, s):
         to = q + (1 << s)
-        return send(blocks.at[0, q], blocks.at[0, to], sem_ps.at[to], sem_pr.at[to], device(0, 1 << s))
-
-    def p_from(q):
-        return send(blocks.at[0, 0], blocks.at[0, q], sem_ps.at[q], sem_pr.at[q], partner)
-
-    def f_copy(q):
-        return send(blocks.at[0, q], blocks.at[1, q], sem_fs.at[q], sem_fr.at[q], partner)
+        return send(blocks.at[0, q, z], blocks.at[0, to, z], sem_ps.at[z, to], sem_pr.at[z, to],
+                    device(0, stage_bit(z, s)))
+
+    def p_from(z, q):
+        return send(blocks.at[0, 0, z], blocks.at[0, q, z], sem_ps.at[z, q], sem_pr.at[z, q], partner)
+
+    def f_copy(z, q):
+        return send(blocks.at[0, q, z], blocks.at[1, q, z], sem_fs.at[z, q], sem_fr.at[z, q], partner)
 
     def each(fn):
         fn(1, 0)
@@ -103,12 +120,14 @@
 
     pl.semaphore_wait(barrier, stages + 1)
     for s in reversed(range(stages)):
-        p_copy(0, s).start()
-    f_copy(0).start()
-
-    lanes = lax.broadcasted_iota(jnp.int32, (half, wide), 1)
+        for z in (0, 1):
+            p_copy(z, 0, s).start()
+    for z in (0, 1):
+        f_copy(z, 0).start()
+
+    lanes = lax.broadcasted_iota(jnp.int32, (quarter, wide), 1)
     first = lanes < dim
-    one = jnp.ones((half, wide), BF16)
+    one = jnp.ones((quarter, wide), BF16)
 
     def tile(pb):
         f = pb.astype(F32)
@@ -124,41 +143,53 @@
         k_bot = jnp.exp(e_bot).astype(BF16)
         return k_top, k_bot
 
-    def absorb(p, q, vec, acc):
-        k_top, k_bot = tile(blocks[p, q, 0:half])
-        if keep:
-            kt[p, q, 0:half] = k_top
-            kt[p, q, half:local] = k_bot
-        v = vec.astype(BF16)
-        acc = acc + jnp.dot(v[:, :half], k_top, preferred_element_type=F32)
-        return acc + jnp.dot(v[:, half:], k_bot, preferred_element_type=F32)
-
-    def unpack(p, q):
-        part = blocks[p, q, half:].astype(F32)
-        hi, mid, lo = (
-            jnp.concatenate([part[i * t_rows + j:i * t_rows + j + 1] for j in range(t_rows)], axis=1)
-            for i in range(3))
-        vec = hi + mid + lo
-        t_all[p, q] = vec
-        return vec
-
-    acc = jnp.zeros((1, local), F32)
-    acc = absorb(0, 0, target, acc)
-    f_copy(0).wait_recv()
-    acc = absorb(1, 0, unpack(1, 0), acc)
+    def at(z, h):
+        return pl.ds(h * half + z * quarter, quarter)
+
+    def absorb(p, q, vec_of, acc):
+        for z in (0, 1):
+            slot = swapped(q) if z else q
+            k_top, k_bot = tile(blocks[p, q, z, 0:quarter])
+            if keep:
+                kt[p, slot, at(z, 0)] = k_top
+                kt[p, slot, at(z, 1)] = k_bot
+            v = jnp.concatenate(vec_of(p, q, z, slot), axis=1)
+            acc = acc + jnp.dot(v, jnp.concatenate([k_top, k_bot], axis=0), preferred_element_type=F32)
+        return acc
+
+    def fresh(p, q, z, slot):
+        part = blocks[p, q, z, quarter:].astype(F32)
+        found = []
+        for h in (0, 1):
+            hi, mid, lo = (
+                jnp.concatenate([part[(2 * i + h) * t_rows + j:(2 * i + h) * t_rows + j + 1] for j in range(t_rows)], axis=1)
+                for i in range(3))
+            t_all[p, slot, :, at(z, h)] = hi + mid + lo
+            found.append(hi.astype(BF16))
+        return found
+
+    def stored(p, q, z, slot):
+        return [t_all[p, slot, :, at(z, h)].astype(BF16) for h in (0, 1)]
+
+    acc = absorb(0, 0, fresh, jnp.zeros((1, local), F32))
 
     def step(q, acc):
-        p_from(q).wait_recv()
-        for s in reversed(range(stages)):
-            @pl.when(q < (1 << s))
-            def _():
-                p_copy(q, s).start()
-        f_copy(q).start()
-        acc = absorb(0, q, unpack(0, q), acc)
-        f_copy(q).wait_recv()
-        return absorb(1, q, unpack(1, q), acc)
+        for z in (0, 1):
+            p_from(z, q).wait_recv()
+            for s in reversed(range(stages)):
+                @pl.when(q < (1 << s))
+                def _():
+                    p_copy(z, q, s).start()
+            f_copy(z, q).start()
+        for z in (0, 1):
+            f_copy(z, q - 1).wait_recv()
+        acc = absorb(0, q, fresh, acc)
+        return absorb(1, q - 1, fresh, acc)
 
     acc = lax.fori_loop(1, half_n, step, acc)
+    for z in (0, 1):
+        f_copy(z, half_n - 1).wait_recv()
+    acc = absorb(1, half_n - 1, fresh, acc)
     weight = ridge[0, 0]
     w_all[0, 0] = acc + weight * target
     t_whole = t_all[...]
@@ -169,12 +200,14 @@
     def _(q):
         w_copy(q).start()
 
-    f_copy(0).wait_send()
-
-    @pl.loop(1, half_n)
-    def _(q):
-        p_from(q).wait_send()
-        f_copy(q).wait_send()
+    for z in (0, 1):
+        f_copy(z, 0).wait_send()
+
+    @pl.loop(1, half_n)
+    def _(q):
+        for z in (0, 1):
+            p_from(z, q).wait_send()
+            f_copy(z, q).wait_send()
 
     @pl.loop(1, half_n)
     def _(q):
@@ -201,7 +234,7 @@
             if keep:
                 acc = acc + jnp.dot(t_all[p, q].astype(BF16), kt[p, q], preferred_element_type=F32)
             else:
-                acc = absorb(p, q, t_all[p, q], acc)
+                acc = absorb(p, q, stored, acc)
         return acc
 
     acc = lax.fori_loop(0, half_n, again, jnp.zeros((1, local), F32))
@@ -223,7 +256,8 @@
     half_n = n // 2
     keep = n * local * local * 2 <= KEEP_BYTES
     kt_shape = (2, half_n, local, local) if keep else (1, 1, 16, 128)
-    t_tile = -(-3 * local // (32 * dim)) * 16
+    quarter = local // 4
+    t_tile = -(-6 * quarter // (32 * dim)) * 16
     dma = pltpu.SemaphoreType.DMA
     vec = jax.ShapeDtypeStruct((1, local), F32)
     coef, res = pl.pallas_call(
@@ -237,7 +271,7 @@
         out_specs=(pl.BlockSpec(memory_space=pltpu.VMEM), pl.BlockSpec(memory_space=pltpu.VMEM)),
         scratch_shapes=[
             pltpu.VMEM((local, dim), BF16),
-            pltpu.VMEM((2, half_n, local // 2 + t_tile, 2 * dim), BF16),
+            pltpu.VMEM((2, half_n, 2, quarter + t_tile, 2 * dim), BF16),
             pltpu.VMEM((2, half_n, 1, local), F32),
             pltpu.VMEM((2, half_n, 1, local), F32),
             pltpu.VMEM((2, half_n, 1, 128), F32),
@@ -245,8 +279,8 @@
             pltpu.VMEM((4 * dim, local), BF16),
             pltpu.VMEM(kt_shape, BF16),
             dma,
-            dma((half_n,)), dma((half_n,)),
-            dma((half_n,)), dma((half_n,)),
+            dma((2, half_n)), dma((2, half_n)),
+            dma((2, half_n)), dma((2, half_n)),
             dma((half_n,)), dma((half_n,)),
             dma((half_n,)), dma((half_n,)),
             dma((2, half_n)), dma((2, half_n)),

time: 55.3 us -> 53.1 us (0.960)
  Pallas kernels: 50.2 us -> 48.1 us
    pallas_call x1, Pallas kernels: 50.2 us -> 48.1 us  [body(): pl.pallas_call(functools.partial(kernel, n, dim, keep), out_shape=(vec, v...]
where the time goes in v3:
time: 53.1 us; the launch traced here: 52.8 us
  Pallas kernels  48.1 us (91%)
  local copies, waits for them, and re-layouts  3.49 us (7%)
  between operations  1.29 us (2%)
    pallas_call x1, Pallas kernels, body(): pl.pallas_call(functools.partial(kernel, n, dim, keep), out_shape=(vec, v...  48.1 us
    unnamed x7, local copies, waits for them, and re-layouts  3.49 us

profile of v3, /device:TPU:0, one launch (start us, length us, event | category | flops | bytes accessed | tf_op | source)
XLA Modules:
  0.0 52.8 jit_solution(13477062712497171843)
XLA Ops:
  1.3 1.6 %copy.5.pts_hbm = bf16[512,64]{1,0:T(8,128)(2,1)} copy(bf16[512,64]{0,1:T(8,128)(2,1)} %param.3) | data formatting | bytes 131072 | tf_op args[0]
  2.9 48.1 %shard_map.50 = (f32[1,512]{1,0:T(1,128)}, f32[1,512]{1,0:T(1,128)}) custom-call(bf16[512,64]{1,0:T(8,128)(2,1)} %copy.5.pts_hbm, f32[1,512]{1,0:T(1,128)} %bitcast.5, f32[1,1]{1,0:T(1,128)} %bitcast.4.ridge), custom_call_target="tpu_custom_call" | custom-call | tf_op jit(solution)/shard_map/pallas_call | solution.py:263
  50.9 0.0 copy-start.1
  50.9 0.7 %copy-done.1 = f32[1,512]{1,0:T(1,128)S(1)} copy-done((f32[1,512]{1,0:T(1,128)S(1)}, f32[1,512]{1,0:T(1,128)}, u32[]{:S(2)}) %copy-start.1) | copy-done | bytes 2072
  51.6 0.0 copy-start
  51.6 0.6 %copy.9 = f32[512]{0:T(512)} copy(f32[512]{0:T(512)S(1)} %bitcast.7) | data formatting | bytes 4096
  52.2 0.1 copy-done
  52.3 0.6 %copy.10 = f32[512]{0:T(512)} copy(f32[512]{0:T(512)S(1)} %bitcast.6) | data formatting | bytes 4096
Async XLA Ops:
  50.9 0.7 %copy-start.1 = (f32[1,512]{1,0:T(1,128)S(1)}, f32[1,512]{1,0:T(1,128)}, u32[]{:S(2)}) copy-start(f32[1,512]{1,0:T(1,128)} %get-tuple-element.4) | copy-start | bytes 6148
  51.6 0.7 %copy-start = (f32[1,512]{1,0:T(1,128)S(1)}, f32[1,512]{1,0:T(1,128)}, u32[]{:S(2)}) copy-start(f32[1,512]{1,0:T(1,128)} %get-tuple-element.5) | copy-start | bytes 6148

commit v4 on v3

--- a/solution.py
+++ b/solution.py
@@ -28,7 +28,7 @@
     def device(p, q):
         d = lax.rem(me + p, 2)
         for s in range(stages):
-            bit = half_n >> s
+            bit = half_n >> (s if s >= stages - 2 else stages - 3 - s)
             d = d + lax.rem(me // bit + q // (1 << s), 2) * bit
         return d
 
@@ -40,11 +40,16 @@
     def swapped(q):
         return q - low * (lax.rem(q // (2 * low), 2) - lax.rem(q // low, 2))
 
+    def turn(i):
+        q = jnp.where(i - 1 < 2 * low, i - 1, i)
+        q = jnp.where(i - 2 < low, i - 2, q)
+        return jnp.where(i == 0, 0, jnp.where(i == 1, low, jnp.where(i == 2, 2 * low, q)))
+
     partner = device(1, 0)
     load = pltpu.make_async_copy(pts_hbm, pts, sem_in)
     load.start()
     barrier = pltpu.get_barrier_semaphore()
-    for dev in [partner] + [device(0, 1 << s) for s in range(stages)]:
+    for dev in [partner, device(0, 3)] + [device(0, 1 << s) for s in range(stages)]:
         pl.semaphore_signal(barrier, inc=1, device_id=(dev,), device_id_type=pl.DeviceIdType.MESH)
 
     target = tgt[...]
@@ -118,10 +123,12 @@
             fn(0, q)
             fn(1, q)
 
-    pl.semaphore_wait(barrier, stages + 1)
+    pl.semaphore_wait(barrier, stages + 2)
     for s in reversed(range(stages)):
         for z in (0, 1):
             p_copy(z, 0, s).start()
+    for z in (0, 1):
+        send(blocks.at[0, 0, z], blocks.at[0, 3, z], sem_ps.at[z, 3], sem_pr.at[z, 3], device(0, 3)).start()
     for z in (0, 1):
         f_copy(z, 0).start()
 
@@ -137,24 +144,24 @@
         hi = pltpu.roll(hi.astype(F32), dim, 1).astype(BF16)
         top = jnp.concatenate([jnp.where(first, pb, hi), jnp.where(first, lo, one)], axis=1)
         bot = jnp.concatenate([jnp.where(first, hi, pb), jnp.where(first, one, lo)], axis=1)
-        e_top = jnp.dot(top, r_a[...], preferred_element_type=F32)
-        k_top = jnp.exp(e_top).astype(BF16)
-        e_bot = jnp.dot(bot, r_b[...], preferred_element_type=F32)
-        k_bot = jnp.exp(e_bot).astype(BF16)
-        return k_top, k_bot
+        return top, bot
 
     def at(z, h):
         return pl.ds(h * half + z * quarter, quarter)
 
     def absorb(p, q, vec_of, acc):
-        for z in (0, 1):
-            slot = swapped(q) if z else q
-            k_top, k_bot = tile(blocks[p, q, z, 0:quarter])
+        slots = (q, swapped(q))
+        tiles = [tile(blocks[p, q, z, 0:quarter]) for z in (0, 1)]
+        vecs = [vec_of(p, q, z, slots[z]) for z in (0, 1)]
+        for h in (0, 1):
+            both = jnp.concatenate([tiles[0][h], tiles[1][h]], axis=0)
+            e = jnp.dot(both, (r_a, r_b)[h][...], preferred_element_type=F32)
+            k = jnp.exp(e).astype(BF16)
             if keep:
-                kt[p, slot, at(z, 0)] = k_top
-                kt[p, slot, at(z, 1)] = k_bot
-            v = jnp.concatenate(vec_of(p, q, z, slot), axis=1)
-            acc = acc + jnp.dot(v, jnp.concatenate([k_top, k_bot], axis=0), preferred_element_type=F32)
+                for z in (0, 1):
+                    kt[p, slots[z], at(z, h)] = k[z * quarter:(z + 1) * quarter]
+            v = jnp.concatenate([vecs[0][h], vecs[1][h]], axis=1)
+            acc = acc + jnp.dot(v, k, preferred_element_type=F32)
         return acc
 
     def fresh(p, q, z, slot):
@@ -173,18 +180,20 @@
 
     acc = absorb(0, 0, fresh, jnp.zeros((1, local), F32))
 
-    def step(q, acc):
+    def step(i, acc):
+        q = turn(i)
+        last = turn(i - 1)
         for z in (0, 1):
             p_from(z, q).wait_recv()
-            for s in reversed(range(stages)):
+            for s in reversed(range(2, stages)):
                 @pl.when(q < (1 << s))
                 def _():
                     p_copy(z, q, s).start()
             f_copy(z, q).start()
         for z in (0, 1):
-            f_copy(z, q - 1).wait_recv()
+            f_copy(z, last).wait_recv()
         acc = absorb(0, q, fresh, acc)
-        return absorb(1, q - 1, fresh, acc)
+        return absorb(1, last, fresh, acc)
 
     acc = lax.fori_loop(1, half_n, step, acc)
     for z in (0, 1):

time: 53.1 us -> 52.6 us (level)
  Pallas kernels: 48.1 us -> 47.5 us
where the time goes in v4:
time: 52.6 us; the launch traced here: 52.3 us
  Pallas kernels  47.5 us (90%)
  local copies, waits for them, and re-layouts  3.49 us (7%)
  between operations  1.29 us (2%)
    pallas_call x1, Pallas kernels, body(): pl.pallas_call(functools.partial(kernel, n, dim, keep), out_shape=(vec, v...  47.5 us
    unnamed x7, local copies, waits for them, and re-layouts  3.49 us

profile of v4, /device:TPU:0, one launch (start us, length us, event | category | flops | bytes accessed | tf_op | source)
XLA Modules:
  0.0 52.3 jit_solution(13829790778481974697)
XLA Ops:
  1.3 1.6 %copy.5.pts_hbm = bf16[512,64]{1,0:T(8,128)(2,1)} copy(bf16[512,64]{0,1:T(8,128)(2,1)} %param.3) | data formatting | bytes 131072 | tf_op args[0]
  2.9 47.5 %shard_map.50 = (f32[1,512]{1,0:T(1,128)}, f32[1,512]{1,0:T(1,128)}) custom-call(bf16[512,64]{1,0:T(8,128)(2,1)} %copy.5.pts_hbm, f32[1,512]{1,0:T(1,128)} %bitcast.5, f32[1,1]{1,0:T(1,128)} %bitcast.4.ridge), custom_call_target="tpu_custom_call" | custom-call | tf_op jit(solution)/shard_map/pallas_call | solution.py:272
  50.4 0.0 copy-start.1
  50.4 0.7 %copy-done.1 = f32[1,512]{1,0:T(1,128)S(1)} copy-done((f32[1,512]{1,0:T(1,128)S(1)}, f32[1,512]{1,0:T(1,128)}, u32[]{:S(2)}) %copy-start.1) | copy-done | bytes 2072
  51.1 0.0 copy-start
  51.1 0.6 %copy.9 = f32[512]{0:T(512)} copy(f32[512]{0:T(512)S(1)} %bitcast.7) | data formatting | bytes 4096
  51.7 0.1 copy-done
  51.8 0.6 %copy.10 = f32[512]{0:T(512)} copy(f32[512]{0:T(512)S(1)} %bitcast.6) | data formatting | bytes 4096
Async XLA Ops:
  50.4 0.7 %copy-start.1 = (f32[1,512]{1,0:T(1,128)S(1)}, f32[1,512]{1,0:T(1,128)}, u32[]{:S(2)}) copy-start(f32[1,512]{1,0:T(1,128)} %get-tuple-element.4) | copy-start | bytes 6148
  51.1 0.7 %copy-start = (f32[1,512]{1,0:T(1,128)S(1)}, f32[1,512]{1,0:T(1,128)}, u32[]{:S(2)}) copy-start(f32[1,512]{1,0:T(1,128)} %get-tuple-element.5) | copy-start | bytes 6148

commit v5 on v4

--- a/solution.py
+++ b/solution.py
@@ -124,11 +124,11 @@
             fn(1, q)
 
     pl.semaphore_wait(barrier, stages + 2)
-    for s in reversed(range(stages)):
+    for z in (0, 1):
+        send(blocks.at[0, 0, z], blocks.at[0, 3, z], sem_ps.at[z, 3], sem_pr.at[z, 3], device(0, 3)).start()
+    for s in range(stages):
         for z in (0, 1):
             p_copy(z, 0, s).start()
-    for z in (0, 1):
-        send(blocks.at[0, 0, z], blocks.at[0, 3, z], sem_ps.at[z, 3], sem_pr.at[z, 3], device(0, 3)).start()
     for z in (0, 1):
         f_copy(z, 0).start()
 

time: 52.6 us -> 52.2 us (level)
  no operation moved by 1% of the time
where the time goes in v5:
time: 52.2 us; the launch traced here: 52 us
  Pallas kernels  47.2 us (90%)
  local copies, waits for them, and re-layouts  3.49 us (7%)
  between operations  1.29 us (2%)
    pallas_call x1, Pallas kernels, body(): pl.pallas_call(functools.partial(kernel, n, dim, keep), out_shape=(vec, v...  47.2 us
    unnamed x7, local copies, waits for them, and re-layouts  3.49 us

profile of v5, /device:TPU:0, one launch (start us, length us, event | category | flops | bytes accessed | tf_op | source)
XLA Modules:
  0.0 52.0 jit_solution(9645614245624298249)
XLA Ops:
  1.3 1.6 %copy.5.pts_hbm = bf16[512,64]{1,0:T(8,128)(2,1)} copy(bf16[512,64]{0,1:T(8,128)(2,1)} %param.3) | data formatting | bytes 131072 | tf_op args[0]
  2.9 47.2 %shard_map.50 = (f32[1,512]{1,0:T(1,128)}, f32[1,512]{1,0:T(1,128)}) custom-call(bf16[512,64]{1,0:T(8,128)(2,1)} %copy.5.pts_hbm, f32[1,512]{1,0:T(1,128)} %bitcast.5, f32[1,1]{1,0:T(1,128)} %bitcast.4.ridge), custom_call_target="tpu_custom_call" | custom-call | tf_op jit(solution)/shard_map/pallas_call | solution.py:272
  50.1 0.0 copy-start.1
  50.1 0.7 %copy-done.1 = f32[1,512]{1,0:T(1,128)S(1)} copy-done((f32[1,512]{1,0:T(1,128)S(1)}, f32[1,512]{1,0:T(1,128)}, u32[]{:S(2)}) %copy-start.1) | copy-done | bytes 2072
  50.7 0.0 copy-start
  50.7 0.6 %copy.9 = f32[512]{0:T(512)} copy(f32[512]{0:T(512)S(1)} %bitcast.7) | data formatting | bytes 4096
  51.3 0.1 copy-done
  51.4 0.6 %copy.10 = f32[512]{0:T(512)} copy(f32[512]{0:T(512)S(1)} %bitcast.6) | data formatting | bytes 4096
Async XLA Ops:
  50.1 0.7 %copy-start.1 = (f32[1,512]{1,0:T(1,128)S(1)}, f32[1,512]{1,0:T(1,128)}, u32[]{:S(2)}) copy-start(f32[1,512]{1,0:T(1,128)} %get-tuple-element.4) | copy-start | bytes 6148
  50.7 0.7 %copy-start = (f32[1,512]{1,0:T(1,128)S(1)}, f32[1,512]{1,0:T(1,128)}, u32[]{:S(2)}) copy-start(f32[1,512]{1,0:T(1,128)} %get-tuple-element.5) | copy-start | bytes 6148
